TPU v7x, 32 devices: a whole 2x2x4 slice. The times are simulated.
32 devices in a mesh: rep: 4 (over z), inst: 8 (over y, x, core).
Axes of the slice: x: 2, y: 2, z: 4, core: 2. Of those that a mesh axis runs over, the one named last changes fastest.
Arguments:
- acts: bfloat16 [32768, 4096], P(('rep', 'inst')), may hold values from -6 to 6
- grad_keys: bfloat16 [32768, 1024], P(('rep', 'inst')), may hold values from -0.0625 to 0.0625
- grad_values: bfloat16 [32768, 1024], P(('rep', 'inst')), may hold values from -0.0625 to 0.0625
- grad_logits: bfloat16 [8, 32768], P(None, ('rep', 'inst')), may hold values from -0.0625 to 0.0625
- order: int32 [32], replicated, may hold values from 0 to 31, each once
- bucket_param: float32 [4, 2048, 1024], P(None, 'inst'), may hold values from -6 to 6
- bucket_m: float32 [4, 2048, 1024], P(None, 'inst'), may hold values from -6 to 6
- bucket_v: float32 [4, 2048, 1024], P(None, 'inst'), may hold values from 0.25 to 4
- router_param: float32 [32, 1024], P('inst'), may hold values from -6 to 6
- router_m: float32 [32, 1024], P('inst'), may hold values from -6 to 6
- router_v: float32 [32, 1024], P('inst'), may hold values from 0.25 to 4
Outputs:
- new_param: float32 [4, 2048, 1024], P(None, 'inst')
- new_moment: float32 [4, 2048, 1024], P(None, 'inst')
- new_second: float32 [4, 2048, 1024], P(None, 'inst')
- router_new_param: float32 [32, 1024], P('inst')
- router_new_moment: float32 [32, 1024], P('inst')
- router_new_second: float32 [32, 1024], P('inst')
Inputs may be any that keep to these rules, and one draw needn't show every extreme that they name: order is a permutation of the 32 row blocks; entries with k * 8 <= s < (k + 1) * 8 fill bucket k.
All inputs are finite; a program needn't handle non-finite values.
Results may differ from a plain program's by a relative error of at most 0.0003.
Values sent between devices are 32-bit elements; how exact they have to be, the bound alone decides.
A program may use at most 256 MiB of HBM per device.

v0:
```python
import jax
import jax.numpy as jnp
from jax import lax
from jax.sharding import PartitionSpec as P

BUCKETS = 4
BLOCK_ROWS = 256


beta_first = 0.9
beta_second = 0.95
step_rate = 0.05
decay_rate = 0.1
epsilon = 1e-08
correct_first = 1.0 - 0.9**10
correct_second = 1.0 - 0.95**10


def contract(left, right):
    return lax.dot_general(
        left, right, (((0,), (0,)), ((), ())), preferred_element_type=jnp.float32
    )


def adamw(grad, param, moment, second):
    moment_new = beta_first * moment + (1.0 - beta_first) * grad
    second_new = beta_second * second + (1.0 - beta_second) * grad * grad
    ratio = moment_new / correct_first / (jnp.sqrt(second_new / correct_second) + epsilon)
    param_new = param - step_rate * (ratio + decay_rate * param)
    return (param_new, moment_new, second_new)


def owner_step(term, param, moment, second):
    share = lax.psum_scatter(term, "inst", scatter_dimension=0, tiled=True)
    total = lax.psum(share, "rep")
    return adamw(total, param, moment, second)


def on_device(
    acts,
    grad_keys,
    grad_values,
    grad_logits,
    order,
    bucket_param,
    bucket_m,
    bucket_v,
    router_param,
    router_m,
    router_v,
):
    per_bucket = order.shape[0] // BUCKETS
    weight_rows = jnp.concatenate([contract(acts, grad_keys), contract(acts, grad_values)], axis=0)
    params_out = []
    moments_out = []
    seconds_out = []
    for bucket in range(BUCKETS):
        pieces = []
        for slot in range(per_bucket):
            block = order[bucket * per_bucket + slot]
            pieces.append(lax.dynamic_slice_in_dim(weight_rows, block * BLOCK_ROWS, BLOCK_ROWS, 0))
        term = jnp.concatenate(pieces, axis=0)
        fresh = owner_step(term, bucket_param[bucket], bucket_m[bucket], bucket_v[bucket])
        params_out.append(fresh[0])
        moments_out.append(fresh[1])
        seconds_out.append(fresh[2])
    router_term = jnp.dot(grad_logits, acts, preferred_element_type=jnp.float32)
    router_term = router_term.reshape(-1, router_param.shape[1])
    router_share = lax.psum_scatter(router_term, "inst", scatter_dimension=0, tiled=True)
    router_total = lax.psum(router_share, "rep")
    router_fresh = adamw(router_total, router_param, router_m, router_v)
    return (
        jnp.stack(params_out),
        jnp.stack(moments_out),
        jnp.stack(seconds_out),
        router_fresh[0],
        router_fresh[1],
        router_fresh[2],
    )


def solution(mesh):
    return jax.shard_map(
        on_device,
        mesh=mesh,
        in_specs=(
            P(("rep", "inst"), None),
            P(("rep", "inst"), None),
            P(("rep", "inst"), None),
            P(None, ("rep", "inst")),
            P(),
            P(None, "inst", None),
            P(None, "inst", None),
            P(None, "inst", None),
            P("inst", None),
            P("inst", None),
            P("inst", None),
        ),
        out_specs=(
            P(None, "inst", None),
            P(None, "inst", None),
            P(None, "inst", None),
            P("inst", None),
            P("inst", None),
            P("inst", None),
        ),
        check_vma=False,
    )
```

profile of v0, /device:TPU:0, one launch (start us, length us, event | category | flops | bytes accessed | tf_op | source)
XLA Modules:
  0.0 602.7 jit_solution(1667637888820862590)
XLA Ops:
  7.2 1.8 fusion.91
  14.1 2.1 fusion.90
  18.2 14.8 %fusion.92 = f32[4096,1024]{1,0:T(8,128)} fusion(bf16[1024,4096]{1,0:T(8,128)(2,1)} %param.11, bf16[1024,1024]{1,0:T(8,128)(2,1)S(1)} %copy-done), kind=kOutput, calls=%fused_computation.178 | convolution fusion | flops 8589934592 | bytes 27262976 | tf_op jit(solution)/shard_map/dot_general | solution.py:20
  33.0 11.5 %fusion.93 = f32[4096,1024]{1,0:T(8,128)} fusion(bf16[1024,4096]{1,0:T(8,128)(2,1)S(1)} %copy-done.4, bf16[1024,1024]{1,0:T(8,128)(2,1)S(1)} %copy-done.16), kind=kOutput, calls=%fused_computation.179 | convolution fusion | flops 8589934592 | bytes 27262976 | tf_op jit(solution)/shard_map/dot_general | solution.py:20
  44.6 1.6 fusion.3
  46.2 4.4 copy-done.2
  50.6 4.8 copy-done.3
  55.7 0.3 fusion.7
  57.1 3.9 fusion.17
  61.0 3.3 copy-done.6
  70.4 2.7 fusion.21
  73.1 3.4 fusion.23
  76.5 1.2 slice-done.12
  77.7 2.0 slice-done.13
  79.7 2.1 slice-done.2
  81.8 1.8 slice-done.3
  83.6 1.4 slice-done.14
  85.0 1.3 slice-done.15
  86.3 1.3 fusion.25
  87.5 1.3 fusion.27
  88.8 1.3 fusion.29
  90.1 1.3 fusion.31
  91.3 2.4 fusion.33
  98.2 2.8 fusion.39
  101.1 3.6 fusion.41
  104.7 1.5 slice-done.17
  106.2 1.3 slice-done.6
  107.5 1.5 slice-done.7
  109.0 1.2 slice-done.18
  110.2 1.3 slice-done.19
  111.4 1.3 fusion.43
  112.7 1.3 fusion.45
  114.0 1.3 fusion.47
  115.3 2.1 fusion.49
  120.6 2.7 fusion.57
  123.3 3.8 fusion.59
  127.2 1.3 slice-done.21
  128.5 1.2 slice-done.10
  129.7 1.2 slice-done.11
  130.9 1.3 slice-done.22
  132.1 1.2 slice-done.23
  133.3 1.3 fusion.61
  134.6 1.3 fusion.63
  135.9 1.3 fusion.1
  137.3 0.6 copy-done.12
  137.9 4.6 fusion.94
  142.5 0.7 reshape.95
  143.3 70.3 %reduce-scatter.7.cloned.1.call-done = f32[256,1024]{1,0:T(8,128)} async-done(((f32[2048,1024]{1,0:T(8,128)}), f32[256,1024]{1,0:T(8,128)}) %reduce-scatter.7.cloned.1.call-update) | async-done | bytes 1048592 | tf_op jit(solution)/shard_map/reduce_scatter | solution.py:34
  213.7 75.0 %reduce-scatter.9.cloned.1.call-done = f32[256,1024]{1,0:T(8,128)} async-done(((f32[2048,1024]{1,0:T(8,128)}), f32[256,1024]{1,0:T(8,128)}) %reduce-scatter.9.cloned.1.call-update) | async-done | bytes 1048592 | tf_op jit(solution)/shard_map/reduce_scatter | solution.py:34
  288.6 74.8 %reduce-scatter.11.cloned.1.call-done = f32[256,1024]{1,0:T(8,128)} async-done(((f32[2048,1024]{1,0:T(8,128)}), f32[256,1024]{1,0:T(8,128)}) %reduce-scatter.11.cloned.1.call-update) | async-done | bytes 1048592 | tf_op jit(solution)/shard_map/reduce_scatter | solution.py:34
  363.5 0.6 dynamic-slice
  364.8 55.6 %all-reduce.5.cloned.1.call-done = f32[32,1024]{1,0:T(8,128)} async-done(((f32[32,1024]{1,0:T(8,128)}), f32[32,1024]{1,0:T(8,128)}) %all-reduce.5.cloned.1.call-update) | async-done | bytes 131088
  420.4 0.8 constant_dynamic-slice_fusion
  421.1 19.5 %psum.39 = f32[4,1024]{1,0:T(4,128)S(1)} all-reduce(f32[4,1024]{1,0:T(4,128)S(1)} %constant_dynamic-slice_fusion), channel_id=1, replica_groups=mesh['rep'=4,'inst'=8] {'rep'}, use_global_device_ids=true, to_apply=%region_9.0 | all-reduce | flops 4096 | bytes 32768 | tf_op jit(solution)/shard_map/psum | solution.py:70
  440.7 0.6 multiply_subtract_fusion
  441.4 136.1 %all-reduce.7.cloned.1.call-done = (f32[256,1024]{1,0:T(8,128)}, f32[256,1024]{1,0:T(8,128)}, f32[256,1024]{1,0:T(8,128)}, f32[256,1024]{1,0:T(8,128)}) async-done(((f32[256,1024]{1,0:T(8,128)}, f32[256,1024]{1,0:T(8,128)}, f32[256,1024]{1,0:T(8,128)}, f32[256,1024]{1,0:T(8,128)}), (f32[256,1024]{1,0:T(8,128)}, f32[256,1024]{1,0:T(8,128)}, f32[256,1024]{1,0:T(8,128)}, ...) | async-done | bytes 4194320 | tf_op jit(solution)/shard_map/psum | solution.py:35
  577.4 5.6 fusion.80
  583.1 0.6 copy-done.7
  583.9 0.3 copy-done.9
  584.2 0.3 copy-done.10
  584.5 0.3 copy-done.11
  584.8 4.7 fusion.79
  589.5 2.6 pad_maximum_fusion.1
  592.1 3.8 pad_maximum_fusion
  (84 shorter events, 2.3 us)
Async XLA Ops:
  7.2 11.0 %copy-start = (bf16[1024,1024]{1,0:T(8,128)(2,1)S(1)}, bf16[1024,1024]{1,0:T(8,128)(2,1)}, u32[]{:S(2)}) copy-start(bf16[1024,1024]{1,0:T(8,128)(2,1)} %param.12) | copy-start | bytes 6291460
  7.2 136.1 %reduce-scatter.5.cloned.1.call-start = ((), (), s32[]{:S(2)}) async-start(), calls=%async_computation.4 | async-start | bytes 9437184 | tf_op jit(solution)/shard_map/reduce_scatter | solution.py:34
  18.2 14.8 %copy-start.4 = (bf16[1024,4096]{1,0:T(8,128)(2,1)S(1)}, bf16[1024,4096]{1,0:T(8,128)(2,1)}, u32[]{:S(2)}) copy-start(bf16[1024,4096]{1,0:T(8,128)(2,1)} %param.11) | copy-start | bytes 25165828
  18.2 14.8 %copy-start.16 = (bf16[1024,1024]{1,0:T(8,128)(2,1)S(1)}, bf16[1024,1024]{1,0:T(8,128)(2,1)}, u32[]{:S(2)}) copy-start(bf16[1024,1024]{1,0:T(8,128)(2,1)} %param.13) | copy-start | bytes 6291460
  44.5 6.1 %copy-start.2 = (f32[4096,1024]{1,0:T(8,128)S(1)}, f32[4096,1024]{1,0:T(8,128)}, u32[]{:S(2)}) copy-start(f32[4096,1024]{1,0:T(8,128)} %fusion.92) | copy-start | bytes 50331652
  44.6 10.9 %copy-start.3 = (f32[4096,1024]{1,0:T(8,128)S(1)}, f32[4096,1024]{1,0:T(8,128)}, u32[]{:S(2)}) copy-start(f32[4096,1024]{1,0:T(8,128)} %fusion.93) | copy-start | bytes 50331652
  61.0 3.3 copy-start.6
  64.3 149.4 %reduce-scatter.7.cloned.1.call-start = ((), (), s32[]{:S(2)}) async-start(), calls=%async_computation.5 | async-start | bytes 9437184 | tf_op jit(solution)/shard_map/reduce_scatter | solution.py:34
  70.3 6.2 %slice-start = ((s8[16777216]{0:T(1024)(128)(4,1)}), s8[4194304]{0:T(1024)(128)(4,1)S(1)}, s32[]{:S(2)}) async-start(s8[16777216]{0:T(1024)(128)(4,1)} %bitcast.155), calls=%async_computation.10 | async-start | bytes 8388608
  70.3 6.2 %slice-start.1 = ((s8[16777216]{0:T(1024)(128)(4,1)}), s8[4194304]{0:T(1024)(128)(4,1)S(1)}, s32[]{:S(2)}) async-start(s8[16777216]{0:T(1024)(128)(4,1)} %bitcast.155), calls=%async_computation.11 | async-start | bytes 8388608
  70.4 7.4 %slice-start.12 = ((s8[16777216]{0:T(1024)(128)(4,1)}), s8[4194304]{0:T(1024)(128)(4,1)S(1)}, s32[]{:S(2)}) async-start(s8[16777216]{0:T(1024)(128)(4,1)} %bitcast.161), calls=%async_computation.22 | async-start | bytes 8388608
  70.4 9.3 %slice-start.13 = ((s8[16777216]{0:T(1024)(128)(4,1)}), s8[4194304]{0:T(1024)(128)(4,1)S(1)}, s32[]{:S(2)}) async-start(s8[16777216]{0:T(1024)(128)(4,1)} %bitcast.161), calls=%async_computation.23 | async-start | bytes 8388608
  73.1 8.6 %slice-start.2 = ((s8[16777216]{0:T(1024)(128)(4,1)}), s8[4194304]{0:T(1024)(128)(4,1)S(1)}, s32[]{:S(2)}) async-start(s8[16777216]{0:T(1024)(128)(4,1)} %bitcast.155), calls=%async_computation.12 | async-start | bytes 8388608
  73.1 10.5 %slice-start.3 = ((s8[16777216]{0:T(1024)(128)(4,1)}), s8[4194304]{0:T(1024)(128)(4,1)S(1)}, s32[]{:S(2)}) async-start(s8[16777216]{0:T(1024)(128)(4,1)} %bitcast.155), calls=%async_computation.13 | async-start | bytes 8388608
  73.1 11.8 %slice-start.14 = ((s8[16777216]{0:T(1024)(128)(4,1)}), s8[4194304]{0:T(1024)(128)(4,1)S(1)}, s32[]{:S(2)}) async-start(s8[16777216]{0:T(1024)(128)(4,1)} %bitcast.161), calls=%async_computation.24 | async-start | bytes 8388608
  73.1 13.2 %slice-start.15 = ((s8[16777216]{0:T(1024)(128)(4,1)}), s8[4194304]{0:T(1024)(128)(4,1)S(1)}, s32[]{:S(2)}) async-start(s8[16777216]{0:T(1024)(128)(4,1)} %bitcast.161), calls=%async_computation.25 | async-start | bytes 8388608
  93.7 194.9 %reduce-scatter.9.cloned.1.call-start = ((), (), s32[]{:S(2)}) async-start(), calls=%async_computation.6 | async-start | bytes 9437184 | tf_op jit(solution)/shard_map/reduce_scatter | solution.py:34
  98.2 6.5 %slice-start.4 = ((s8[16777216]{0:T(1024)(128)(4,1)}), s8[4194304]{0:T(1024)(128)(4,1)S(1)}, s32[]{:S(2)}) async-start(s8[16777216]{0:T(1024)(128)(4,1)} %bitcast.157), calls=%async_computation.14 | async-start | bytes 8388608
  98.2 6.5 %slice-start.5 = ((s8[16777216]{0:T(1024)(128)(4,1)}), s8[4194304]{0:T(1024)(128)(4,1)S(1)}, s32[]{:S(2)}) async-start(s8[16777216]{0:T(1024)(128)(4,1)} %bitcast.157), calls=%async_computation.15 | async-start | bytes 8388608
  98.2 6.5 %slice-start.16 = ((s8[16777216]{0:T(1024)(128)(4,1)}), s8[4194304]{0:T(1024)(128)(4,1)S(1)}, s32[]{:S(2)}) async-start(s8[16777216]{0:T(1024)(128)(4,1)} %bitcast.163), calls=%async_computation.26 | async-start | bytes 8388608
  98.2 8.0 %slice-start.17 = ((s8[16777216]{0:T(1024)(128)(4,1)}), s8[4194304]{0:T(1024)(128)(4,1)S(1)}, s32[]{:S(2)}) async-start(s8[16777216]{0:T(1024)(128)(4,1)} %bitcast.163), calls=%async_computation.27 | async-start | bytes 8388608
  101.0 6.4 %slice-start.6 = ((s8[16777216]{0:T(1024)(128)(4,1)}), s8[4194304]{0:T(1024)(128)(4,1)S(1)}, s32[]{:S(2)}) async-start(s8[16777216]{0:T(1024)(128)(4,1)} %bitcast.157), calls=%async_computation.16 | async-start | bytes 8388608
  101.1 7.9 %slice-start.7 = ((s8[16777216]{0:T(1024)(128)(4,1)}), s8[4194304]{0:T(1024)(128)(4,1)S(1)}, s32[]{:S(2)}) async-start(s8[16777216]{0:T(1024)(128)(4,1)} %bitcast.157), calls=%async_computation.17 | async-start | bytes 8388608
  101.1 9.1 %slice-start.18 = ((s8[16777216]{0:T(1024)(128)(4,1)}), s8[4194304]{0:T(1024)(128)(4,1)S(1)}, s32[]{:S(2)}) async-start(s8[16777216]{0:T(1024)(128)(4,1)} %bitcast.163), calls=%async_computation.28 | async-start | bytes 8388608
  101.1 10.4 %slice-start.19 = ((s8[16777216]{0:T(1024)(128)(4,1)}), s8[4194304]{0:T(1024)(128)(4,1)S(1)}, s32[]{:S(2)}) async-start(s8[16777216]{0:T(1024)(128)(4,1)} %bitcast.163), calls=%async_computation.29 | async-start | bytes 8388608
  117.4 246.1 %reduce-scatter.11.cloned.1.call-start = ((), (), s32[]{:S(2)}) async-start(), calls=%async_computation.7 | async-start | bytes 9437184 | tf_op jit(solution)/shard_map/reduce_scatter | solution.py:34
  120.5 6.6 %slice-start.8 = ((s8[16777216]{0:T(1024)(128)(4,1)}), s8[4194304]{0:T(1024)(128)(4,1)S(1)}, s32[]{:S(2)}) async-start(s8[16777216]{0:T(1024)(128)(4,1)} %bitcast.159), calls=%async_computation.18 | async-start | bytes 8388608
  120.5 6.6 %slice-start.9 = ((s8[16777216]{0:T(1024)(128)(4,1)}), s8[4194304]{0:T(1024)(128)(4,1)S(1)}, s32[]{:S(2)}) async-start(s8[16777216]{0:T(1024)(128)(4,1)} %bitcast.159), calls=%async_computation.19 | async-start | bytes 8388608
  120.5 6.6 %slice-start.20 = ((s8[16777216]{0:T(1024)(128)(4,1)}), s8[4194304]{0:T(1024)(128)(4,1)S(1)}, s32[]{:S(2)}) async-start(s8[16777216]{0:T(1024)(128)(4,1)} %bitcast.165), calls=%async_computation.30 | async-start | bytes 8388608
  120.6 7.9 %slice-start.21 = ((s8[16777216]{0:T(1024)(128)(4,1)}), s8[4194304]{0:T(1024)(128)(4,1)S(1)}, s32[]{:S(2)}) async-start(s8[16777216]{0:T(1024)(128)(4,1)} %bitcast.165), calls=%async_computation.31 | async-start | bytes 8388608
  123.3 6.4 %slice-start.10 = ((s8[16777216]{0:T(1024)(128)(4,1)}), s8[4194304]{0:T(1024)(128)(4,1)S(1)}, s32[]{:S(2)}) async-start(s8[16777216]{0:T(1024)(128)(4,1)} %bitcast.159), calls=%async_computation.20 | async-start | bytes 8388608
  123.3 7.6 %slice-start.11 = ((s8[16777216]{0:T(1024)(128)(4,1)}), s8[4194304]{0:T(1024)(128)(4,1)S(1)}, s32[]{:S(2)}) async-start(s8[16777216]{0:T(1024)(128)(4,1)} %bitcast.159), calls=%async_computation.21 | async-start | bytes 8388608
  123.3 8.8 %slice-start.22 = ((s8[16777216]{0:T(1024)(128)(4,1)}), s8[4194304]{0:T(1024)(128)(4,1)S(1)}, s32[]{:S(2)}) async-start(s8[16777216]{0:T(1024)(128)(4,1)} %bitcast.165), calls=%async_computation.32 | async-start | bytes 8388608
  123.3 10.0 %slice-start.23 = ((s8[16777216]{0:T(1024)(128)(4,1)}), s8[4194304]{0:T(1024)(128)(4,1)S(1)}, s32[]{:S(2)}) async-start(s8[16777216]{0:T(1024)(128)(4,1)} %bitcast.165), calls=%async_computation.33 | async-start | bytes 8388608
  137.1 0.7 copy-start.12
  137.2 226.3 %copy-start.17 = (u32[32]{0:T(128)S(1)}, u32[32]{0:T(128)}, u32[]{:S(2)}) copy-start(u32[32]{0:T(128)} %constant.74) | copy-start | bytes 388
  137.2 303.5 %copy-start.13 = (f32[4,1024]{1,0:T(4,128)S(1)}, f32[4,1024]{1,0:T(4,128)}, u32[]{:S(2)}) copy-start(f32[4,1024]{1,0:T(4,128)} %param.19) | copy-start | bytes 49156
  137.2 303.5 %copy-start.14 = (f32[4,1024]{1,0:T(4,128)S(1)}, f32[4,1024]{1,0:T(4,128)}, u32[]{:S(2)}) copy-start(f32[4,1024]{1,0:T(4,128)} %param.20) | copy-start | bytes 49156
  137.2 303.5 %copy-start.15 = (f32[4,1024]{1,0:T(4,128)S(1)}, f32[4,1024]{1,0:T(4,128)}, u32[]{:S(2)}) copy-start(f32[4,1024]{1,0:T(4,128)} %param.21) | copy-start | bytes 49156
  137.2 283.2 %all-reduce.5.cloned.1.call-start = ((), (), s32[]{:S(2)}) async-start(), calls=%async_computation.8 | async-start | bytes 262144
  143.2 434.2 %all-reduce.7.cloned.1.call-start = ((), (), s32[]{:S(2)}) async-start(), calls=%async_computation.9 | async-start | bytes 8388608 | tf_op jit(solution)/shard_map/psum | solution.py:35
  577.4 5.6 copy-start.5
  577.4 6.2 %copy-start.7 = (f32[4,256,1024]{2,1,0:T(8,128)S(1)}, f32[4,256,1024]{2,1,0:T(8,128)}, u32[]{:S(2)}) copy-start(f32[4,256,1024]{2,1,0:T(8,128)} %param.18) | copy-start | bytes 12582916
  577.4 6.4 %copy-start.8 = (f32[256,1024]{1,0:T(8,128)S(1)}, f32[256,1024]{1,0:T(8,128)}, u32[]{:S(2)}) copy-start(f32[256,1024]{1,0:T(8,128)} %get-tuple-element.6) | copy-start | bytes 3145732
  577.4 6.7 %copy-start.9 = (f32[256,1024]{1,0:T(8,128)S(1)}, f32[256,1024]{1,0:T(8,128)}, u32[]{:S(2)}) copy-start(f32[256,1024]{1,0:T(8,128)} %get-tuple-element.7) | copy-start | bytes 3145732
  577.4 7.0 %copy-start.10 = (f32[256,1024]{1,0:T(8,128)S(1)}, f32[256,1024]{1,0:T(8,128)}, u32[]{:S(2)}) copy-start(f32[256,1024]{1,0:T(8,128)} %get-tuple-element.8) | copy-start | bytes 3145732
  577.4 7.3 %copy-start.11 = (f32[256,1024]{1,0:T(8,128)S(1)}, f32[256,1024]{1,0:T(8,128)}, u32[]{:S(2)}) copy-start(f32[256,1024]{1,0:T(8,128)} %get-tuple-element.9) | copy-start | bytes 3145732
  592.1 3.8 copy-start.1
Sparse Core Ops, SparseCore 0:
  64.4 74.2 reduce-scatter.4
  142.1 71.4 reduce-scatter.6
  217.1 71.4 reduce-scatter.8
  292.0 71.4 reduce-scatter.10
  366.9 53.3 all-reduce.4
  422.8 154.5 all-reduce.6
where the time goes:
time: 604 us; the launch traced here: 603 us
  waiting for transfers between devices  412 us (68%)
  other arithmetic  60.9 us (10%)
  local copies, waits for them, and re-layouts  43.5 us (7%)
  between operations  35.4 us (6%)
  matrix products  31 us (5%)
  blocking collectives  19.5 us (3%)
    reduce_scatter x4, waiting for transfers between devices, owner_step(): share = lax.psum_scatter(term, 'inst', scatter_dimension=0, tiled=True)  220 us
    psum x1, waiting for transfers between devices, owner_step(): total = lax.psum(share, 'rep')  136 us
    unnamed x7, waiting for transfers between devices  55.7 us
    unnamed x86, local copies, waits for them, and re-layouts  38.9 us
    unnamed x28, other arithmetic  33.9 us
    dot_general x2, matrix products, contract(): lax.dot_general(left, right, (((0,), (0,)), ((), ())), preferred_element_...  26.3 us
    psum x1, blocking collectives, on_device(): router_total = lax.psum(router_share, 'rep')  19.5 us
  transfers between devices with their start and end apart: 6, of which 5 were waited for; matrix products, arithmetic and copies ran while one was open for 7% of the time, Pallas kernels for 0%

commit v1 on v0

v1 whole, which is shorter than its diff:
```python
import functools

import jax
import jax.numpy as jnp
from jax import lax
from jax.experimental import pallas as pl
from jax.experimental.pallas import tpu as pltpu
from jax.sharding import PartitionSpec as P

MESH = pl.DeviceIdType.MESH
BUCKETS = 4
BLOCK_ROWS = 256
COLS = 128
LAG = 2


beta_first = 0.9
beta_second = 0.95
step_rate = 0.05
decay_rate = 0.1
epsilon = 1e-08
correct_first = 1.0 - 0.9**10
correct_second = 1.0 - 0.95**10


def adamw(grad, param, moment, second):
    moment_new = beta_first * moment + (1.0 - beta_first) * grad
    second_new = beta_second * second + (1.0 - beta_second) * grad * grad
    ratio = moment_new / correct_first / (jnp.sqrt(second_new / correct_second) + epsilon)
    param_new = param - step_rate * (ratio + decay_rate * param)
    return (param_new, moment_new, second_new)


def when_between(p, count, body):
    @pl.when(jnp.logical_and(p >= 0, p < count))
    def _():
        body(p)


class Lane:
    def __init__(self, n_inst, n_rep, dims, root, parts, send, recv, halves, lefts, rights, finish):
        self.n_inst, self.n_rep, self.dims, self.root = n_inst, n_rep, dims, root
        self.parts, self.send, self.recv = parts, send, recv
        self.halves, self.lefts, self.rights, self.finish = halves, lefts, rights, finish
        self.me = lax.axis_index("inst")
        self.rep = lax.axis_index("rep")
        self.stages = len(dims)
        self.base = 1 + LAG * (self.stages - 1)
        self.top = self.base + LAG * max(root, n_rep - 1 - root)

    def partner(self, bit):
        return self.me + (1 - 2 * ((self.me // 2**bit) % 2)) * 2**bit

    def owner(self, q):
        index = self.me
        for at, bit in enumerate(self.dims):
            if (q >> (self.stages - 1 - at)) & 1:
                index = index + (1 - 2 * ((self.me // 2**bit) % 2)) * 2**bit
        return index

    def copy(self, src, dst, stage, p, **device):
        return pltpu.make_async_remote_copy(
            src_ref=src,
            dst_ref=dst,
            send_sem=self.send.at[stage, p],
            recv_sem=self.recv.at[stage, p],
            device_id=device,
            device_id_type=MESH,
        )

    def half_copy(self, stage, p):
        count = self.n_inst >> (stage + 1)
        source = self.parts(p) if stage == 0 else self.halves(stage - 1, p)
        return self.copy(
            source.at[pl.ds(count, count)],
            self.halves(stage, p),
            stage,
            p,
            inst=self.partner(self.dims[stage]),
        )

    def add_half(self, stage, p):
        self.half_copy(stage, p).wait()
        count = self.n_inst >> (stage + 1)
        source = self.parts(p) if stage == 0 else self.halves(stage - 1, p)
        into = self.halves(stage, p)
        into[...] += source[pl.ds(0, count)]

    def total(self, p):
        return self.halves(self.stages - 1, p)

    def to_right(self, src, p):
        return self.copy(src, self.lefts(p), self.stages, p, rep=self.rep + 1)

    def to_left(self, src, p):
        return self.copy(src, self.rights(p), self.stages + 1, p, rep=self.rep - 1)

    def reduce_ends(self, p):
        if self.root > 0:

            @pl.when(self.rep == 0)
            def _():
                self.to_right(self.total(p), p).start()

        if self.root < self.n_rep - 1:

            @pl.when(self.rep == self.n_rep - 1)
            def _():
                self.to_left(self.total(p), p).start()

    def from_left(self, p):
        self.to_right(self.total(p), p).wait_recv()

    def from_right(self, p):
        self.to_left(self.total(p), p).wait_recv()

    def reduce_inner(self, t, count):
        rep, root, last = self.rep, self.root, self.n_rep - 1
        if root > 1:
            p = t - self.base - LAG * rep

            @pl.when((rep > 0) & (rep < root) & (p >= 0) & (p < count))
            def _():
                self.from_left(p)
                total = self.total(p)
                total[...] += self.lefts(p)[...]
                self.to_right(total, p).start()

        if root < last - 1:
            p2 = t - self.base - LAG * (last - rep)

            @pl.when((rep > root) & (rep < last) & (p2 >= 0) & (p2 < count))
            def _():
                self.from_right(p2)
                total = self.total(p2)
                total[...] += self.rights(p2)[...]
                self.to_left(total, p2).start()

    def at_root(self, t, count):
        p = t - self.top

        @pl.when((self.rep == self.root) & (p >= 0) & (p < count))
        def _():
            total = self.total(p)
            if self.root > 0:
                self.from_left(p)
                total[...] += self.lefts(p)[...]
            if self.root < self.n_rep - 1:
                self.from_right(p)
                total[...] += self.rights(p)[...]
            if self.root > 0:
                self.to_left(total, p).start()
            if self.root < self.n_rep - 1:
                self.to_right(total, p).start()
            self.finish(total, p)

    def spread(self, t, count):
        rep, root, last = self.rep, self.root, self.n_rep - 1
        if root > 0:
            p = t - self.top - LAG * (root - rep)

            @pl.when((rep < root) & (p >= 0) & (p < count))
            def _():
                self.from_right(p)
                if root > 1:

                    @pl.when(rep > 0)
                    def _():
                        self.to_left(self.rights(p), p).start()

                self.finish(self.rights(p), p)

        if root < last:
            p2 = t - self.top - LAG * (rep - root)

            @pl.when((rep > root) & (p2 >= 0) & (p2 < count))
            def _():
                self.from_left(p2)
                if root < last - 1:

                    @pl.when(rep < last)
                    def _():
                        self.to_right(self.lefts(p2), p2).start()

                self.finish(self.lefts(p2), p2)

    def settle(self, p):
        @pl.when(self.rep < self.n_rep - 1)
        def _():
            self.to_right(self.total(p), p).wait_send()

        @pl.when(self.rep > 0)
        def _():
            self.to_left(self.total(p), p).wait_send()

    def last_step(self):
        return self.top + LAG * max(self.root, self.n_rep - 1 - self.root)


def kernel(
    n_inst,
    n_rep,
    order,
    acts,
    keys,
    values,
    logits,
    out,
    router_out,
    slabs,
    turned,
    router_all,
    parts,
    router_parts,
    load,
    *scratch,
):
    bits = n_inst.bit_length() - 1
    rows = parts.shape[-1]
    width = router_parts.shape[-1]
    per_bucket = order.shape[0] // BUCKETS
    column_blocks = acts.shape[1] // BLOCK_ROWS
    chunks = keys.shape[1] // COLS
    count = chunks * BUCKETS // 2
    halves = scratch[:bits]
    router_halves = scratch[bits : 2 * bits]
    lefts, rights, router_lefts, router_rights = scratch[2 * bits : 2 * bits + 4]
    sends, recvs, router_sends, router_recvs = scratch[2 * bits + 4 :]

    def finish(kind):
        def body(ref, p):
            bucket = 2 * (p // chunks) + kind
            start = pl.multiple_of((p % chunks) * COLS, COLS)
            out[bucket, :, pl.ds(start, COLS)] = ref[0].T

        return body

    def router_finish(ref, p):
        router_out[...] = ref[0]

    forward = [0] + list(range(1, bits))
    backward = [0] + list(range(bits - 1, 0, -1))
    lanes = []
    for kind, dims in enumerate((forward, backward)):
        lanes.append(
            Lane(
                n_inst,
                n_rep,
                dims,
                ((n_rep - 1) // 2, n_rep // 2)[kind],
                lambda p, kind=kind: parts.at[kind, p % 2],
                sends.at[kind],
                recvs.at[kind],
                lambda stage, p, kind=kind: halves[stage].at[kind, p],
                lambda p, kind=kind: lefts.at[kind, p],
                lambda p, kind=kind: rights.at[kind, p],
                finish(kind),
            )
        )
    router = Lane(
        n_inst,
        n_rep,
        forward,
        (n_rep - 1) // 2,
        lambda p: router_parts,
        router_sends,
        router_recvs,
        lambda stage, p: router_halves[stage],
        lambda p: router_lefts,
        lambda p: router_rights,
        router_finish,
    )
    me, rep = lax.axis_index("inst"), lax.axis_index("rep")

    loads = [
        pltpu.make_async_copy(acts.at[:, pl.ds(at * rows, rows)], slabs.at[at], load.at[at])
        for at in range(slabs.shape[0])
    ]
    for copy in loads:
        copy.start()

    barrier = pltpu.get_barrier_semaphore()
    for bit in range(bits):
        pl.semaphore_signal(
            barrier, inc=1, device_id={"inst": router.partner(bit)}, device_id_type=MESH
        )

    @pl.when(rep > 0)
    def _():
        pl.semaphore_signal(barrier, inc=1, device_id={"rep": rep - 1}, device_id_type=MESH)

    @pl.when(rep < n_rep - 1)
    def _():
        pl.semaphore_signal(barrier, inc=1, device_id={"rep": rep + 1}, device_id_type=MESH)

    ends = jnp.where(rep > 0, 1, 0) + jnp.where(rep < n_rep - 1, 1, 0)
    pl.semaphore_wait(barrier, bits + ends)
    for copy in loads:
        copy.wait()

    def products(p):
        start = pl.multiple_of((p % chunks) * COLS, COLS)
        turned[0] = keys[:, pl.ds(start, COLS)].T
        turned[1] = values[:, pl.ds(start, COLS)].T
        for kind, lane in enumerate(lanes):
            bucket = 2 * (p // chunks) + kind
            for q in reversed(range(n_inst)):
                first = lane.owner(q) * rows
                block = order[bucket * per_bucket + first // BLOCK_ROWS]
                at = lax.rem(block, column_blocks) * (BLOCK_ROWS // rows) + first % BLOCK_ROWS // rows
                parts[kind, p % 2, q] = jnp.dot(
                    turned[lax.div(block, column_blocks)],
                    slabs[at],
                    preferred_element_type=jnp.float32,
                )
            lane.half_copy(0, p).start()

    def router_products(p):
        for at in range(slabs.shape[0]):
            router_all[:, pl.ds(at * rows, rows)] = jnp.dot(
                logits[...], slabs[at], preferred_element_type=jnp.float32
            )
        for q in range(n_inst):
            first = router.owner(q) * width
            router_parts[q] = router_all[
                pl.ds(first // acts.shape[1], 1),
                pl.ds(pl.multiple_of(first % acts.shape[1], width), width),
            ]
        router.half_copy(0, 0).start()

    both = [(lane, count) for lane in lanes] + [(router, 1)]

    def step(t, carry):
        when_between(t, count, products)
        when_between(t, 1, router_products)
        for stage in range(bits):
            lag = 1 + LAG * stage
            for lane, most in both:

                def body(p, lane=lane, stage=stage):
                    lane.add_half(stage, p)
                    if stage < bits - 1:
                        lane.half_copy(stage + 1, p).start()
                    else:
                        lane.reduce_ends(p)

                when_between(t - lag, most, body)
        for lane, most in both:
            lane.reduce_inner(t, most)
            lane.at_root(t, most)
            lane.spread(t, most)
        return carry

    steps = count + max(lane.last_step() for lane, _ in both)
    lax.fori_loop(0, steps, step, 0)

    def close(p, carry):
        for lane in lanes:
            lane.settle(p)
        return carry

    lax.fori_loop(0, count, close, 0)
    router.settle(0)


def summed(order, acts, keys, values, logits, n_inst, n_rep, bucket_rows, router_size):
    bits = n_inst.bit_length() - 1
    rows = bucket_rows // n_inst
    width = router_size // n_inst
    kv = keys.shape[1]
    count = kv // COLS * BUCKETS // 2
    vmem = pl.BlockSpec(memory_space=pltpu.VMEM)
    f32 = jnp.float32
    scratch = [
        pltpu.VMEM((acts.shape[1] // rows, acts.shape[0], rows), acts.dtype),
        pltpu.VMEM((2, COLS, acts.shape[0]), acts.dtype),
        pltpu.VMEM((logits.shape[0], acts.shape[1]), f32),
        pltpu.VMEM((2, 2, n_inst, COLS, rows), f32),
        pltpu.VMEM((n_inst, 1, width), f32),
        pltpu.SemaphoreType.DMA((acts.shape[1] // rows,)),
    ]
    scratch += [pltpu.VMEM((2, count, n_inst >> (s + 1), COLS, rows), f32) for s in range(bits)]
    scratch += [pltpu.VMEM((n_inst >> (s + 1), 1, width), f32) for s in range(bits)]
    scratch += [pltpu.VMEM((2, count, 1, COLS, rows), f32)] * 2
    scratch += [pltpu.VMEM((1, 1, width), f32)] * 2
    scratch += [pltpu.SemaphoreType.DMA((2, bits + 2, count))] * 2
    scratch += [pltpu.SemaphoreType.DMA((bits + 2, 1))] * 2
    return pl.pallas_call(
        functools.partial(kernel, n_inst, n_rep),
        out_shape=(
            jax.ShapeDtypeStruct((BUCKETS, rows, kv), f32),
            jax.ShapeDtypeStruct((1, width), f32),
        ),
        in_specs=[
            pl.BlockSpec(memory_space=pltpu.SMEM),
            pl.BlockSpec(memory_space=pl.ANY),
            vmem,
            vmem,
            vmem,
        ],
        out_specs=(vmem, vmem),
        scratch_shapes=scratch,
        compiler_params=pltpu.CompilerParams(
            collective_id=0, has_side_effects=True, vmem_limit_bytes=67043328
        ),
        cost_estimate=pl.CostEstimate(
            flops=4 * acts.shape[0] * acts.shape[1] * kv,
            bytes_accessed=16 * 2**20,
            transcendentals=0,
        ),
    )(order, acts, keys, values, logits)


def on_device(
    n_inst,
    n_rep,
    acts,
    grad_keys,
    grad_values,
    grad_logits,
    order,
    bucket_param,
    bucket_m,
    bucket_v,
    router_param,
    router_m,
    router_v,
):
    total, router_total = summed(
        order,
        acts,
        grad_keys,
        grad_values,
        grad_logits,
        n_inst,
        n_rep,
        bucket_param.shape[1] * n_inst,
        router_param.size * n_inst,
    )
    fresh = adamw(total, bucket_param, bucket_m, bucket_v)
    router_fresh = adamw(router_total.reshape(router_param.shape), router_param, router_m, router_v)
    return fresh + router_fresh


def solution(mesh):
    return jax.shard_map(
        functools.partial(on_device, mesh.shape["inst"], mesh.shape["rep"]),
        mesh=mesh,
        in_specs=(
            P(("rep", "inst"), None),
            P(("rep", "inst"), None),
            P(("rep", "inst"), None),
            P(None, ("rep", "inst")),
            P(),
            P(None, "inst", None),
            P(None, "inst", None),
            P(None, "inst", None),
            P("inst", None),
            P("inst", None),
            P("inst", None),
        ),
        out_specs=(
            P(None, "inst", None),
            P(None, "inst", None),
            P(None, "inst", None),
            P("inst", None),
            P("inst", None),
            P("inst", None),
        ),
        check_vma=False,
    )
```

time: 604 us -> 210 us (0.35)
  waiting for transfers between devices: 412 us -> 0 us
  Pallas kernels: 0 us -> 196 us
  other arithmetic: 60.9 us -> 12.1 us
  local copies, waits for them, and re-layouts: 43.5 us -> 0.55 us
  between operations: 35.4 us -> 0.71 us
  matrix products: 31 us -> 0 us
  blocking collectives: 19.5 us -> 0 us
    reduce_scatter x4 -> x0, waiting for transfers between devices: 220 us -> none  [owner_step(): share = lax.psum_scatter(term, 'inst', scatter_dimension=0, tiled=True)]
    pallas_call x0 -> x1, Pallas kernels: none -> 196 us  [summed(): pl.pallas_call(functools.partial(kernel, n_inst, n_rep), out_shape=(jax.S...]
    psum x1 -> x0, waiting for transfers between devices: 136 us -> none  [owner_step(): total = lax.psum(share, 'rep')]
    unnamed x7 -> x0, waiting for transfers between devices: 55.7 us -> none
    unnamed x86 -> x8, local copies, waits for them, and re-layouts: 38.9 us -> 0.02 us
    unnamed x28 -> x0, other arithmetic: 33.9 us -> none
    dot_general x3 -> x0, matrix products: 31 us -> none  [the longest x2 26.3 us: contract(): lax.dot_general(left, right, (((0,), (0,)), ((), ())), preferred_element_...]
    psum x1 -> x0, blocking collectives: 19.5 us -> none  [on_device(): router_total = lax.psum(router_share, 'rep')]
  transfers between devices with their start and end apart: 6 -> 0, of which waited for: 5 -> 0; matrix products, arithmetic and copies ran while one was open for 7% -> 0% of each run, Pallas kernels for 0% -> 0%
where the time goes in v1:
time: 210 us; the launch traced here: 209 us
  Pallas kernels  196 us (93%)
  other arithmetic  12.1 us (6%)
    pallas_call x1, Pallas kernels, summed(): pl.pallas_call(functools.partial(kernel, n_inst, n_rep), out_shape=(jax.S...  196 us
    sub x2, other arithmetic, adamw(): param_new = param - step_rate * (ratio + decay_rate * param)  11.4 us

profile of v1, /device:TPU:0, one launch (start us, length us, event | category | flops | bytes accessed | tf_op | source)
XLA Modules:
  0.0 209.4 jit_solution(18152847175505340882)
XLA Ops:
  0.6 196.1 %shard_map.154 = (f32[4,256,1024]{2,1,0:T(8,128)}, f32[1,4096]{1,0:T(1,128)}) custom-call(s32[32]{0:T(128)} %order.1, bf16[1024,4096]{1,0:T(8,128)(2,1)} %acts.1, bf16[1024,1024]{1,0:T(8,128)(2,1)} %keys.1, bf16[1024,1024]{1,0:T(8,128)(2,1)} %values.1, bf16[8,1024]{1,0:T(8,128)(2,1)} %logits.1), custom_call_target="tpu_custom_call" | custom-call | flops 17179869184 | bytes 16777216 | tf_op jit(solution)/shard_map/pallas_call | solution.py:388
  196.7 0.0 copy-start.3
  196.7 0.0 copy-start
  196.7 0.0 copy-start.1
  196.8 0.0 copy-start.2
  196.8 10.8 %multiply_subtract_fusion = (f32[4,256,1024]{2,1,0:T(8,128)}, f32[4,256,1024]{2,1,0:T(8,128)}, f32[4,256,1024]{2,1,0:T(8,128)}) fusion(f32[4,256,1024]{2,1,0:T(8,128)} %param.16, f32[4,256,1024]{2,1,0:T(8,128)} %get-tuple-element.8, f32[4,256,1024]{2,1,0:T(8,128)} %param.17, f32[4,256,1024]{2,1,0:T(8,128)} %param.18), kind=kLoop, calls=%fused_computation.2 | loop fusion | flops 15728640 | bytes 29360128 | tf_op jit(solution)/shard_map/sub | solution.py:30
  207.5 0.5 broadcast.31
  208.1 0.0 copy-done.3
  208.1 0.7 reduce.3
  208.8 0.0 copy-done
  208.8 0.0 copy-done.1
  208.8 0.0 copy-done.2
  208.8 0.6 multiply_subtract_fusion.1
  (1 shorter events, 0.0 us)
Async XLA Ops:
  196.7 11.3 %copy-start.3 = (f32[1,4096]{1,0:T(1,128)S(1)}, f32[1,4096]{1,0:T(1,128)}, u32[]{:S(2)}) copy-start(f32[1,4096]{1,0:T(1,128)} %get-tuple-element.9) | copy-start | bytes 49156
  196.7 12.0 %copy-start = (f32[4,1024]{1,0:T(4,128)S(1)}, f32[4,1024]{1,0:T(4,128)}, u32[]{:S(2)}) copy-start(f32[4,1024]{1,0:T(4,128)} %param.19) | copy-start | bytes 49156
  196.7 12.0 %copy-start.1 = (f32[4,1024]{1,0:T(4,128)S(1)}, f32[4,1024]{1,0:T(4,128)}, u32[]{:S(2)}) copy-start(f32[4,1024]{1,0:T(4,128)} %param.20) | copy-start | bytes 49156
  196.8 12.0 %copy-start.2 = (f32[4,1024]{1,0:T(4,128)S(1)}, f32[4,1024]{1,0:T(4,128)}, u32[]{:S(2)}) copy-start(f32[4,1024]{1,0:T(4,128)} %param.21) | copy-start | bytes 49156

commit v2 on v1

--- a/solution.py
+++ b/solution.py
@@ -11,7 +11,8 @@
 BUCKETS = 4
 BLOCK_ROWS = 256
 COLS = 128
-LAG = 2
+LAG = 1
+SPLIT = 2
 
 
 beta_first = 0.9
@@ -38,15 +39,16 @@
 
 
 class Lane:
-    def __init__(self, n_inst, n_rep, dims, root, parts, send, recv, halves, lefts, rights, finish):
-        self.n_inst, self.n_rep, self.dims, self.root = n_inst, n_rep, dims, root
+    def __init__(self, n_inst, n_rep, dims, parts, send, recv, halves, lefts, rights, finish):
+        self.n_inst, self.n_rep, self.dims = n_inst, n_rep, dims
         self.parts, self.send, self.recv = parts, send, recv
         self.halves, self.lefts, self.rights, self.finish = halves, lefts, rights, finish
         self.me = lax.axis_index("inst")
         self.rep = lax.axis_index("rep")
         self.stages = len(dims)
         self.base = 1 + LAG * (self.stages - 1)
-        self.top = self.base + LAG * max(root, n_rep - 1 - root)
+        self.left = n_rep // 2 - 1
+        self.top = self.base + LAG * (self.left + 1)
 
     def partner(self, bit):
         return self.me + (1 - 2 * ((self.me // 2**bit) % 2)) * 2**bit
@@ -96,14 +98,12 @@
         return self.copy(src, self.rights(p), self.stages + 1, p, rep=self.rep - 1)
 
     def reduce_ends(self, p):
-        if self.root > 0:
+        if self.left > 0:
 
             @pl.when(self.rep == 0)
             def _():
                 self.to_right(self.total(p), p).start()
 
-        if self.root < self.n_rep - 1:
-
             @pl.when(self.rep == self.n_rep - 1)
             def _():
                 self.to_left(self.total(p), p).start()
@@ -114,75 +114,75 @@
     def from_right(self, p):
         self.to_left(self.total(p), p).wait_recv()
 
-    def reduce_inner(self, t, count):
-        rep, root, last = self.rep, self.root, self.n_rep - 1
-        if root > 1:
-            p = t - self.base - LAG * rep
-
-            @pl.when((rep > 0) & (rep < root) & (p >= 0) & (p < count))
-            def _():
-                self.from_left(p)
-                total = self.total(p)
-                total[...] += self.lefts(p)[...]
-                self.to_right(total, p).start()
-
-        if root < last - 1:
-            p2 = t - self.base - LAG * (last - rep)
-
-            @pl.when((rep > root) & (rep < last) & (p2 >= 0) & (p2 < count))
-            def _():
-                self.from_right(p2)
-                total = self.total(p2)
-                total[...] += self.rights(p2)[...]
-                self.to_left(total, p2).start()
-
-    def at_root(self, t, count):
-        p = t - self.top
-
-        @pl.when((self.rep == self.root) & (p >= 0) & (p < count))
-        def _():
+    def reduce(self, t, count):
+        rep, last = self.rep, self.n_rep - 1
+
+        def towards_right(p):
             total = self.total(p)
-            if self.root > 0:
+            if self.left > 0:
                 self.from_left(p)
                 total[...] += self.lefts(p)[...]
-            if self.root < self.n_rep - 1:
+            self.to_right(total, p).start()
+
+        def towards_left(p):
+            total = self.total(p)
+            if self.left > 0:
                 self.from_right(p)
                 total[...] += self.rights(p)[...]
-            if self.root > 0:
-                self.to_left(total, p).start()
-            if self.root < self.n_rep - 1:
-                self.to_right(total, p).start()
-            self.finish(total, p)
+            self.to_left(total, p).start()
+
+        first = min(1, self.left)
+        p = t - self.base - LAG * rep
+
+        @pl.when((rep >= first) & (rep <= self.left) & (p >= 0) & (p < count))
+        def _():
+            towards_right(p)
+
+        p2 = t - self.base - LAG * (last - rep)
+
+        @pl.when((rep > self.left) & (rep <= last - first) & (p2 >= 0) & (p2 < count))
+        def _():
+            towards_left(p2)
 
     def spread(self, t, count):
-        rep, root, last = self.rep, self.root, self.n_rep - 1
-        if root > 0:
-            p = t - self.top - LAG * (root - rep)
-
-            @pl.when((rep < root) & (p >= 0) & (p < count))
+        rep, left, last = self.rep, self.left, self.n_rep - 1
+        p = t - self.top - LAG * (left - rep)
+
+        @pl.when((rep <= left) & (p >= 0) & (p < count))
+        def _():
+            self.from_right(p)
+            whole = self.rights(p)
+
+            @pl.when(rep == left)
             def _():
-                self.from_right(p)
-                if root > 1:
-
-                    @pl.when(rep > 0)
-                    def _():
-                        self.to_left(self.rights(p), p).start()
-
-                self.finish(self.rights(p), p)
-
-        if root < last:
-            p2 = t - self.top - LAG * (rep - root)
-
-            @pl.when((rep > root) & (p2 >= 0) & (p2 < count))
+                whole[...] += self.total(p)[...]
+
+            if left > 0:
+
+                @pl.when(rep > 0)
+                def _():
+                    self.to_left(whole, p).start()
+
+            self.finish(whole, p)
+
+        p2 = t - self.top - LAG * (rep - left - 1)
+
+        @pl.when((rep > left) & (p2 >= 0) & (p2 < count))
+        def _():
+            self.from_left(p2)
+            whole = self.lefts(p2)
+
+            @pl.when(rep == left + 1)
             def _():
-                self.from_left(p2)
-                if root < last - 1:
-
-                    @pl.when(rep < last)
-                    def _():
-                        self.to_right(self.lefts(p2), p2).start()
-
-                self.finish(self.lefts(p2), p2)
+                whole[...] += self.total(p2)[...]
+
+            if left > 0:
+
+                @pl.when(rep < last)
+                def _():
+                    self.to_right(whole, p2).start()
+
+            self.finish(whole, p2)
 
     def settle(self, p):
         @pl.when(self.rep < self.n_rep - 1)
@@ -194,7 +194,7 @@
             self.to_left(self.total(p), p).wait_send()
 
     def last_step(self):
-        return self.top + LAG * max(self.root, self.n_rep - 1 - self.root)
+        return self.top + LAG * self.left
 
 
 def kernel(
@@ -216,12 +216,14 @@
     *scratch,
 ):
     bits = n_inst.bit_length() - 1
-    rows = parts.shape[-1]
+    rows = slabs.shape[-1]
+    short = parts.shape[-1]
     width = router_parts.shape[-1]
     per_bucket = order.shape[0] // BUCKETS
     column_blocks = acts.shape[1] // BLOCK_ROWS
     chunks = keys.shape[1] // COLS
-    count = chunks * BUCKETS // 2
+    split = rows // parts.shape[-1]
+    count = chunks * split * BUCKETS // 2
     halves = scratch[:bits]
     router_halves = scratch[bits : 2 * bits]
     lefts, rights, router_lefts, router_rights = scratch[2 * bits : 2 * bits + 4]
@@ -229,9 +231,11 @@
 
     def finish(kind):
         def body(ref, p):
-            bucket = 2 * (p // chunks) + kind
-            start = pl.multiple_of((p % chunks) * COLS, COLS)
-            out[bucket, :, pl.ds(start, COLS)] = ref[0].T
+            chunk = p // split
+            bucket = 2 * (chunk // chunks) + kind
+            start = pl.multiple_of((chunk % chunks) * COLS, COLS)
+            top = pl.multiple_of((p % split) * short, short)
+            out[bucket, pl.ds(top, short), pl.ds(start, COLS)] = ref[0].T
 
         return body
 
@@ -247,8 +251,7 @@
                 n_inst,
                 n_rep,
                 dims,
-                ((n_rep - 1) // 2, n_rep // 2)[kind],
-                lambda p, kind=kind: parts.at[kind, p % 2],
+                lambda p, kind=kind: parts.at[kind, p % (2 * split)],
                 sends.at[kind],
                 recvs.at[kind],
                 lambda stage, p, kind=kind: halves[stage].at[kind, p],
@@ -261,7 +264,6 @@
         n_inst,
         n_rep,
         forward,
-        (n_rep - 1) // 2,
         lambda p: router_parts,
         router_sends,
         router_recvs,
@@ -298,22 +300,26 @@
     for copy in loads:
         copy.wait()
 
-    def products(p):
-        start = pl.multiple_of((p % chunks) * COLS, COLS)
+    def products(chunk):
+        start = pl.multiple_of((chunk % chunks) * COLS, COLS)
         turned[0] = keys[:, pl.ds(start, COLS)].T
         turned[1] = values[:, pl.ds(start, COLS)].T
         for kind, lane in enumerate(lanes):
-            bucket = 2 * (p // chunks) + kind
+            bucket = 2 * (chunk // chunks) + kind
             for q in reversed(range(n_inst)):
                 first = lane.owner(q) * rows
                 block = order[bucket * per_bucket + first // BLOCK_ROWS]
                 at = lax.rem(block, column_blocks) * (BLOCK_ROWS // rows) + first % BLOCK_ROWS // rows
-                parts[kind, p % 2, q] = jnp.dot(
+                full = jnp.dot(
                     turned[lax.div(block, column_blocks)],
                     slabs[at],
                     preferred_element_type=jnp.float32,
                 )
-            lane.half_copy(0, p).start()
+                for part in range(split):
+                    slot = (chunk % 2) * split + part
+                    parts[kind, slot, q] = full[:, part * short : (part + 1) * short]
+            for part in range(split):
+                lane.half_copy(0, chunk * split + part).start()
 
     def router_products(p):
         for at in range(slabs.shape[0]):
@@ -331,7 +337,10 @@
     both = [(lane, count) for lane in lanes] + [(router, 1)]
 
     def step(t, carry):
-        when_between(t, count, products)
+        @pl.when((t % split == 0) & (t < count))
+        def _():
+            products(t // split)
+
         when_between(t, 1, router_products)
         for stage in range(bits):
             lag = 1 + LAG * stage
@@ -346,8 +355,7 @@
 
                 when_between(t - lag, most, body)
         for lane, most in both:
-            lane.reduce_inner(t, most)
-            lane.at_root(t, most)
+            lane.reduce(t, most)
             lane.spread(t, most)
         return carry
 
@@ -368,20 +376,22 @@
     rows = bucket_rows // n_inst
     width = router_size // n_inst
     kv = keys.shape[1]
-    count = kv // COLS * BUCKETS // 2
+    split = max(1, min(SPLIT, rows // 128))
+    short = rows // split
+    count = kv // COLS * split * BUCKETS // 2
     vmem = pl.BlockSpec(memory_space=pltpu.VMEM)
     f32 = jnp.float32
     scratch = [
         pltpu.VMEM((acts.shape[1] // rows, acts.shape[0], rows), acts.dtype),
         pltpu.VMEM((2, COLS, acts.shape[0]), acts.dtype),
         pltpu.VMEM((logits.shape[0], acts.shape[1]), f32),
-        pltpu.VMEM((2, 2, n_inst, COLS, rows), f32),
+        pltpu.VMEM((2, 2 * split, n_inst, COLS, short), f32),
         pltpu.VMEM((n_inst, 1, width), f32),
         pltpu.SemaphoreType.DMA((acts.shape[1] // rows,)),
     ]
-    scratch += [pltpu.VMEM((2, count, n_inst >> (s + 1), COLS, rows), f32) for s in range(bits)]
+    scratch += [pltpu.VMEM((2, count, n_inst >> (s + 1), COLS, short), f32) for s in range(bits)]
     scratch += [pltpu.VMEM((n_inst >> (s + 1), 1, width), f32) for s in range(bits)]
-    scratch += [pltpu.VMEM((2, count, 1, COLS, rows), f32)] * 2
+    scratch += [pltpu.VMEM((2, count, 1, COLS, short), f32)] * 2
     scratch += [pltpu.VMEM((1, 1, width), f32)] * 2
     scratch += [pltpu.SemaphoreType.DMA((2, bits + 2, count))] * 2
     scratch += [pltpu.SemaphoreType.DMA((bits + 2, 1))] * 2

time: 210 us -> 189 us (0.900)
  Pallas kernels: 196 us -> 176 us
    pallas_call x1, Pallas kernels: 196 us -> 176 us  [summed(): pl.pallas_call(functools.partial(kernel, n_inst, n_rep), out_shape=(jax.S...]
where the time goes in v2:
time: 189 us
  Pallas kernels  176 us (93%)
  other arithmetic  12.1 us (6%)
    pallas_call x1, Pallas kernels, summed(): pl.pallas_call(functools.partial(kernel, n_inst, n_rep), out_shape=(jax.S...  176 us
    sub x2, other arithmetic, adamw(): param_new = param - step_rate * (ratio + decay_rate * param)  11.4 us

profile of v2, /device:TPU:0, one launch (start us, length us, event | category | flops | bytes accessed | tf_op | source)
XLA Modules:
  0.0 189.2 jit_solution(12934459962628788235)
XLA Ops:
  0.6 175.8 %shard_map.154 = (f32[4,256,1024]{2,1,0:T(8,128)}, f32[1,4096]{1,0:T(1,128)}) custom-call(s32[32]{0:T(128)} %order.1, bf16[1024,4096]{1,0:T(8,128)(2,1)} %acts.1, bf16[1024,1024]{1,0:T(8,128)(2,1)} %keys.1, bf16[1024,1024]{1,0:T(8,128)(2,1)} %values.1, bf16[8,1024]{1,0:T(8,128)(2,1)} %logits.1), custom_call_target="tpu_custom_call" | custom-call | flops 17179869184 | bytes 16777216 | tf_op jit(solution)/shard_map/pallas_call | solution.py:398
  176.5 0.0 copy-start.3
  176.5 0.0 copy-start
  176.5 0.0 copy-start.1
  176.5 0.0 copy-start.2
  176.5 10.8 %multiply_subtract_fusion = (f32[4,256,1024]{2,1,0:T(8,128)}, f32[4,256,1024]{2,1,0:T(8,128)}, f32[4,256,1024]{2,1,0:T(8,128)}) fusion(f32[4,256,1024]{2,1,0:T(8,128)} %param.16, f32[4,256,1024]{2,1,0:T(8,128)} %get-tuple-element.8, f32[4,256,1024]{2,1,0:T(8,128)} %param.17, f32[4,256,1024]{2,1,0:T(8,128)} %param.18), kind=kLoop, calls=%fused_computation.2 | loop fusion | flops 15728640 | bytes 29360128 | tf_op jit(solution)/shard_map/sub | solution.py:31
  187.3 0.5 broadcast.31
  187.8 0.0 copy-done.3
  187.8 0.7 reduce.3
  188.5 0.0 copy-done
  188.5 0.0 copy-done.1
  188.5 0.0 copy-done.2
  188.5 0.6 multiply_subtract_fusion.1
  (1 shorter events, 0.0 us)
Async XLA Ops:
  176.5 11.3 %copy-start.3 = (f32[1,4096]{1,0:T(1,128)S(1)}, f32[1,4096]{1,0:T(1,128)}, u32[]{:S(2)}) copy-start(f32[1,4096]{1,0:T(1,128)} %get-tuple-element.9) | copy-start | bytes 49156
  176.5 12.0 %copy-start = (f32[4,1024]{1,0:T(4,128)S(1)}, f32[4,1024]{1,0:T(4,128)}, u32[]{:S(2)}) copy-start(f32[4,1024]{1,0:T(4,128)} %param.19) | copy-start | bytes 49156
  176.5 12.0 %copy-start.1 = (f32[4,1024]{1,0:T(4,128)S(1)}, f32[4,1024]{1,0:T(4,128)}, u32[]{:S(2)}) copy-start(f32[4,1024]{1,0:T(4,128)} %param.20) | copy-start | bytes 49156
  176.5 12.0 %copy-start.2 = (f32[4,1024]{1,0:T(4,128)S(1)}, f32[4,1024]{1,0:T(4,128)}, u32[]{:S(2)}) copy-start(f32[4,1024]{1,0:T(4,128)} %param.21) | copy-start | bytes 49156
